TPU v7x, 128 devices: a whole 4x4x4 slice. The times are simulated.
128 devices in a mesh: seq: 32 (over y, z, core), dp: 4 (over x).
Axes of the slice: x: 4, y: 4, z: 4, core: 2. Of those that a mesh axis runs over, the one named last changes fastest.
Arguments:
- query_input: bfloat16 [4, 16384, 2048], P('dp', 'seq'), may hold values from -6 to 6
- key_input: bfloat16 [4, 16384, 2048], P('dp', 'seq'), may hold values from -6 to 6
- value_input: bfloat16 [4, 16384, 2048], P('dp', 'seq'), may hold values from -6 to 6
- grad_output: bfloat16 [4, 16384, 2048], P('dp', 'seq'), may hold values from -6 to 6
- out_weight: bfloat16 [2048, 2048], P(('seq', 'dp')), may hold values from -0.125 to 0.125
- norm_gain: float32 [2048], replicated, may hold values from 0.1 to 1.9
Outputs:
- result: bfloat16 [4, 16384, 2048], P('dp', 'seq')
- grad_query: bfloat16 [4, 16384, 2048], P('dp', 'seq')
- grad_key: bfloat16 [4, 16384, 2048], P('dp', 'seq')
- grad_value: bfloat16 [4, 16384, 2048], P('dp', 'seq')
- grad_weight: float32 [2048, 2048], P(('seq', 'dp'))
All inputs are finite; a program needn't handle non-finite values.
Results may differ from a plain program's by a relative error of at most 0.015.
Values may be sent and summed in bfloat16 or wider, within the bound.
No kernel may reach another device: no remote copies, remote signals or barrier semaphores. Data moves between devices by JAX's collectives and lax.ppermute only.
A program may use at most 192 MiB of HBM per device.

v0:
```python
import jax
import jax.numpy as jnp
from jax import lax
from jax.sharding import Mesh
from jax.sharding import PartitionSpec as P

HEADS = 16
HEAD_DIM = 128
BLOCK = 512
SEQ = ("seq_0", "seq_1", "seq_2")
SEQ_DP = ("seq_0", "seq_1", "seq_2", "dp")
epsilon = 1e-06


def filled_with(shard, identity):
    return jnp.zeros_like(shard) + jnp.asarray(identity, shard.dtype)


def entering(shard, axes, combine, identity, reverse):
    before = start = filled_with(shard, identity)
    total = shard
    for axis in reversed(axes):
        peers, index = (lax.axis_size(axis), lax.axis_index(axis))
        pieces = lax.all_gather(total, axis)
        inside, total = (start, start)
        for k in reversed(range(peers)) if reverse else range(peers):
            passed = k > index if reverse else k < index
            total = combine(total, pieces[k])
            inside = jnp.where(passed, total, inside)
        before = combine(inside, before)
    return before


def split_up(shard, dim, peers):
    shape = shard.shape
    blocks = shard.reshape(*shape[:dim], peers, shape[dim] // peers, *shape[dim + 1 :])
    return jnp.moveaxis(blocks, dim, 0)


def scatter_pairs(shard, chips, core, dim):
    sizes = (lax.axis_size(chips), lax.axis_size(core))
    blocks = split_up(shard, dim, sizes[0] * sizes[1])
    inside = blocks.shape[1:]
    blocks = blocks.reshape(*sizes, *inside).swapaxes(0, 1).reshape(-1, *inside)
    blocks = lax.psum_scatter(blocks, core, scatter_dimension=0, tiled=True)
    return lax.psum_scatter(blocks, chips, scatter_dimension=0, tiled=True)[0]


def sent_and_summed(shard, axis, dim):
    peers = lax.axis_size(axis)
    blocks = lax.all_to_all(split_up(shard, dim, peers), axis, 0, 0, tiled=True)
    return jnp.sum(blocks.astype(jnp.float32), axis=0)


def silu_slope(inputs):
    sigmoid_value = jax.nn.sigmoid(inputs)
    return sigmoid_value * (1.0 + inputs * (1.0 - sigmoid_value))


def add_states(earlier, following):
    return earlier + following


def causal_product(left, right):
    scores = jnp.einsum("ihd,jhd->hij", left, right, preferred_element_type=jnp.float32)
    length_now = left.shape[0]
    causal = jnp.arange(length_now)[:, None] >= jnp.arange(length_now)[None, :]
    return jnp.where(causal[None], scores, 0.0)


def product(form, left, right):
    return jnp.einsum(form, left, right, preferred_element_type=jnp.float32)


def forward_parts(query_block, key_block, value_block, state_low):
    score_block = causal_product(query_block, key_block).astype(jnp.bfloat16)
    inside = product("hij,jhe->ihe", score_block, value_block)
    carried = product("ihd,hde->ihe", query_block, state_low)
    return (inside + carried, score_block)


def forward_only(items):
    return forward_parts(*items)[0]


def backward_core(
    query_block, key_block, value_block, grad_block, state_low, later_low, score_block
):
    grad_scores = causal_product(grad_block, value_block).astype(jnp.bfloat16)
    grad_fq = product("hij,jhd->ihd", grad_scores, key_block) + product(
        "ihe,hde->ihd", grad_block, state_low
    )
    grad_fk = product("hij,ihd->jhd", grad_scores, query_block) + product(
        "jhe,hde->jhd", value_block, later_low
    )
    grad_fv = product("hij,ihe->jhe", score_block, grad_block) + product(
        "jhd,hde->jhe", key_block, later_low
    )
    return (grad_fq, grad_fk, grad_fv)


def backward_again(items):
    query_block, key_block = (items[0], items[1])
    score_block = causal_product(query_block, key_block).astype(jnp.bfloat16)
    return backward_core(*items + (score_block,))


def shards(query_input, key_input, value_input, grad_output, out_weight, norm_gain):
    tokens = query_input.shape[1]
    feature_count = query_input.shape[2]
    blocks = tokens // BLOCK
    query_raw = query_input[0].astype(jnp.float32)
    key_raw = key_input[0].astype(jnp.float32)
    feat_query = jax.nn.silu(query_raw).astype(jnp.bfloat16).reshape(blocks, BLOCK, HEADS, HEAD_DIM)
    feat_key = jax.nn.silu(key_raw).astype(jnp.bfloat16).reshape(blocks, BLOCK, HEADS, HEAD_DIM)
    value_blocks = value_input[0].reshape(blocks, BLOCK, HEADS, HEAD_DIM)
    zero_state = jnp.zeros((HEADS, HEAD_DIM, HEAD_DIM), jnp.float32)
    block_kv = product("bjhd,bjhe->bhde", feat_key, value_blocks)
    local_incl = jnp.cumsum(block_kv, axis=0)
    incoming = entering(local_incl[-1], SEQ, add_states, zero_state, False)
    prefix = (incoming[None] + (local_incl - block_kv)).astype(jnp.bfloat16)
    full_weight = lax.all_gather(out_weight, SEQ_DP, axis=0, tiled=True)
    attention = lax.map(forward_only, (feat_query, feat_key, value_blocks, prefix))
    attention = attention.reshape(tokens, feature_count)
    radius = jnp.sqrt(jnp.mean(attention * attention, axis=-1, keepdims=True) + epsilon)
    normed = attention / radius
    mixed = (normed * norm_gain).astype(jnp.bfloat16)
    result = jnp.dot(mixed, full_weight, preferred_element_type=jnp.float32).astype(jnp.bfloat16)
    grad_result = grad_output[0]
    grad_mixed = lax.dot_general(
        grad_result, full_weight, (((1,), (1,)), ((), ())), preferred_element_type=jnp.float32
    )
    grad_hat = grad_mixed * norm_gain
    grad_att = (grad_hat - normed * jnp.mean(grad_hat * normed, axis=-1, keepdims=True)) / radius
    grad_att = grad_att.astype(jnp.bfloat16).reshape(blocks, BLOCK, HEADS, HEAD_DIM)
    block_grad = product("bihd,bihe->bhde", feat_query, grad_att)
    suffix_incl = jnp.cumsum(block_grad[::-1], axis=0)[::-1]
    incoming_later = entering(suffix_incl[0], SEQ, add_states, zero_state, True)
    later = (incoming_later[None] + (suffix_incl - block_grad)).astype(jnp.bfloat16)
    grad_fq, grad_fk, grad_fv = lax.map(
        backward_again, (feat_query, feat_key, value_blocks, grad_att, prefix, later)
    )
    grad_query = (grad_fq.reshape(tokens, feature_count) * silu_slope(query_raw)).astype(
        jnp.bfloat16
    )
    grad_key = (grad_fk.reshape(tokens, feature_count) * silu_slope(key_raw)).astype(jnp.bfloat16)
    grad_value = grad_fv.reshape(tokens, feature_count).astype(jnp.bfloat16)
    partial_value = scatter_pairs(
        lax.dot_general(
            mixed, grad_result, (((0,), (0,)), ((), ())), preferred_element_type=jnp.float32
        ).astype(jnp.bfloat16),
        ("seq_0", "seq_1"),
        "seq_2",
        0,
    ).astype(jnp.float32)
    grad_weight = sent_and_summed(partial_value.astype(jnp.bfloat16), "dp", 0)
    return (result[None], grad_query[None], grad_key[None], grad_value[None], grad_weight)


def solution(mesh):
    torus = Mesh(mesh.devices.reshape(4, 4, 2, mesh.shape["dp"]), ("seq_0", "seq_1", "seq_2", "dp"))
    placed = (
        P("dp", SEQ, None),
        P("dp", SEQ, None),
        P("dp", SEQ, None),
        P("dp", SEQ, None),
        P(SEQ_DP, None),
        P(),
    )
    return jax.shard_map(
        shards,
        mesh=torus,
        in_specs=placed,
        out_specs=(
            P("dp", SEQ, None),
            P("dp", SEQ, None),
            P("dp", SEQ, None),
            P("dp", SEQ, None),
            P(SEQ_DP, None),
        ),
        check_vma=False,
    )
```

profile of v0, /device:TPU:2, one launch (start us, length us, event | category | flops | bytes accessed | tf_op | source)
XLA Modules:
  0.0 469.6 jit_solution(1941817382321238800)
XLA Ops:
  7.2 2.3 copy.88
  11.1 1.6 multiply_convert_fusion.2
  12.7 1.3 copy-done.9
  14.1 2.4 fusion.23
  16.5 15.8 %all-gather.18.cloned.1.call-done = f32[32,128,128]{2,1,0:T(8,128)} async-done(((f32[16,128,128]{2,1,0:T(8,128)}), f32[32,128,128]{2,1,0:T(8,128)}) %all-gather.18.cloned.1.call-update) | async-done | bytes 2097168 | tf_op jit(solution)/shard_map/all_gather | solution.py:24
  32.3 2.6 slice_add_fusion.13
  35.1 49.8 %all-gather.22.cloned.1.call-done = f32[64,128,128]{2,1,0:T(8,128)} async-done(((f32[16,128,128]{2,1,0:T(8,128)}), f32[64,128,128]{2,1,0:T(8,128)}) %all-gather.22.cloned.1.call-update) | async-done | bytes 4194320 | tf_op jit(solution)/shard_map/all_gather | solution.py:24
  84.9 3.4 fusion.36
  89.4 2.1 convert_bitcast_fusion.1
  92.6 1.6 multiply_convert_fusion.3
  94.2 1.3 copy-done.5
  95.5 2.5 select_convert_fusion.1
  98.0 3.4 copy-done.4
  101.5 4.9 %fusion.19 = f32[16,512,128]{1,2,0:T(8,128)} fusion(bf16[16,512,512]{2,1,0:T(8,128)(2,1)S(1)} %select_convert_fusion.1, bf16[512,16,128]{2,1,0:T(8,128)(2,1)S(1)} %bitcast.110), kind=kOutput, calls=%fused_computation.41 | convolution fusion | flops 1073741824 | bytes 14680064 | tf_op jit(solution)/shard_map/while/body/eval_jaxpr/hij,jhe->ihe/dot_general | solution.py:72
  106.4 30.5 %all-gather.12.cloned.1.call-done = f32[4,16,128,128]{3,2,1,0:T(8,128)} async-done(((f32[1,16,128,128]{3,2,1,0:T(8,128)}), f32[4,16,128,128]{3,2,1,0:T(8,128)}) %all-gather.12.cloned.1.call-update) | async-done | bytes 4194320 | tf_op jit(solution)/shard_map/all_gather | solution.py:24
  136.9 5.8 %fusion.35 = bf16[16,128,128]{2,1,0:T(8,128)(2,1)S(1)} fusion(f32[4,16,128,128]{3,2,1,0:T(8,128)} %all-gather.12.cloned.1.call-done, f32[16,128,128]{2,1,0:T(8,128)} %fusion.23, f32[64,128,128]{2,1,0:T(8,128)} %all-gather.22.cloned.1.call-done, f32[32,128,128]{2,1,0:T(8,128)} %all-gather.18.cloned.1.call-done, pred[]{:T(512)S(6)} %gt.35, pred[]{:T(512)S(6)} %gt.36, ...), kind=kLoop, calls=%fused_computation.65 | loop fusion | flops 5767168 | bytes 12058634 | tf_op jit(solution)/shard_map/convert_element_type | solution.py:121
  143.1 2.8 multiply_reduce_fusion.1
  145.8 5.6 %copy.64 = f32[512,2048]{1,0:T(8,128)} copy(f32[512,2048]{0,1:T(8,128)} %bitcast.106) | data formatting | bytes 8388608 | tf_op jit(solution)/shard_map/reshape | solution.py:124
  151.4 57.2 %all-gather.14.cloned.1.call-done = bf16[2048,2048]{1,0:T(8,128)(2,1)} async-done(((bf16[16,2048]{1,0:T(8,128)(2,1)}), bf16[2048,2048]{1,0:T(8,128)(2,1)}) %all-gather.14.cloned.1.call-update) | async-done | bytes 8388624 | tf_op jit(solution)/shard_map/all_gather | solution.py:122
  208.7 9.3 %multiply_reduce_fusion = (f32[512]{0:T(512)S(1)}, f32[512,2048]{1,0:T(8,128)S(1)}) fusion(f32[2048]{0:T(1024)S(1)} %copy-done.24, f32[512,2048]{1,0:T(8,128)} %copy.64, f32[512]{0:T(512)S(1)} %add_sqrt_fusion, bf16[2048,2048]{1,0:T(8,128)(2,1)} %all-gather.14.cloned.1.call-done, bf16[1,512,2048]{2,1,0:T(8,128)(2,1)S(1)} %copy-done), kind=kOutput, calls=%fused_computation.27 | convolution fusion | flops 4299161088 | bytes 18886656 | tf_op jit(solution)/shard_map/dot_general | solution.py:130
  218.0 2.2 divide_convert_fusion
  220.2 3.9 copy.85
  224.1 4.0 fusion.39
  228.2 12.2 %all-gather.20.cloned.1.call-done = f32[32,128,128]{2,1,0:T(8,128)} async-done(((f32[16,128,128]{2,1,0:T(8,128)}), f32[32,128,128]{2,1,0:T(8,128)}) %all-gather.20.cloned.1.call-update) | async-done | bytes 2097168 | tf_op jit(solution)/shard_map/all_gather | solution.py:24
  240.3 2.7 slice_add_fusion.6
  243.1 2.6 multiply_convert_fusion
  245.7 6.8 %convolution_convert_fusion = bf16[2048,2048]{1,0:T(8,128)(2,1)} fusion(bf16[512,2048]{0,1:T(8,128)(2,1)S(1)} %bitcast.118, bf16[1,512,2048]{2,1,0:T(8,128)(2,1)S(1)} %copy-done), kind=kOutput, calls=%fused_computation.2 | convolution fusion | flops 4299161600 | bytes 12582912 | tf_op jit(solution)/shard_map/dot_general | solution.py:149
  252.5 9.0 %copy.77 = bf16[16,2,64,2048]{3,2,0,1:T(8,128)(2,1)} copy(bf16[16,2,64,2048]{3,2,1,0:T(8,128)(2,1)} %bitcast.117) | data formatting | bytes 16777216 | tf_op jit(solution)/shard_map/reshape;reshape | solution.py:44
  261.6 31.3 %all-gather.24.cloned.1.call-done = f32[64,128,128]{2,1,0:T(8,128)} async-done(((f32[16,128,128]{2,1,0:T(8,128)}), f32[64,128,128]{2,1,0:T(8,128)}) %all-gather.24.cloned.1.call-update) | async-done | bytes 4194320 | tf_op jit(solution)/shard_map/all_gather | solution.py:24
  292.9 3.5 fusion.30
  296.4 18.4 %reduce-scatter.5.cloned.1.call-done = bf16[16,64,2048]{2,1,0:T(8,128)(2,1)} async-done(((bf16[32,64,2048]{2,1,0:T(8,128)(2,1)}), bf16[16,64,2048]{2,1,0:T(8,128)(2,1)}) %reduce-scatter.5.cloned.1.call-update) | async-done | bytes 4194320 | tf_op jit(solution)/shard_map/reduce_scatter | solution.py:45
  314.8 4.6 select_convert_fusion
  319.5 4.9 %fusion.37 = f32[16,128,512]{2,1,0:T(8,128)} fusion(bf16[512,16,128]{2,0,1:T(8,128)(2,1)S(1)} %copy-done.11, bf16[16,512,512]{2,1,0:T(8,128)(2,1)S(1)} %select_convert_fusion), kind=kOutput, calls=%fused_computation.81 | convolution fusion | flops 1073741824 | bytes 14680064 | tf_op jit(solution)/shard_map/while/body/eval_jaxpr/hij,jhd->ihd/dot_general | solution.py:72
  324.3 4.9 %convolution_add_fusion.1 = f32[16,128,512]{2,1,0:T(8,128)} fusion(f32[16,128,512]{2,1,0:T(8,128)} %fusion.37, bf16[16,128,128]{2,1,0:T(8,128)(2,1)S(1)} %fusion.35, bf16[512,16,128]{0,2,1:T(8,128)(2,1)S(1)} %bitcast.105), kind=kOutput, calls=%fused_computation.35 | convolution fusion | flops 269484032 | bytes 11010048 | tf_op jit(solution)/shard_map/while/body/eval_jaxpr/ihe,hde->ihd/dot_general | solution.py:72
  329.2 5.8 %copy.69 = f32[1,512,2048]{2,1,0:T(8,128)} copy(f32[1,512,2048]{1,2,0:T(8,128)} %bitcast.113) | data formatting | bytes 8388608 | tf_op jit(solution)/shard_map/reshape | solution.py:143
  335.0 7.7 %fusion.40 = f32[16,128,512]{2,1,0:T(8,128)} fusion(bf16[512,16,128]{0,2,1:T(8,128)(2,1)} %bitcast.103, bf16[16,512,512]{2,1,0:T(8,128)(2,1)} %copy-done.4), kind=kOutput, calls=%fused_computation.84 | convolution fusion | flops 1073741824 | bytes 14680064 | tf_op jit(solution)/shard_map/while/body/eval_jaxpr/hij,ihe->jhe/dot_general | solution.py:72
  343.7 3.6 fusion.38
  347.3 1.9 slice-done.1
  349.2 5.8 %fusion.14 = bf16[1,512,2048]{2,1,0:T(8,128)(2,1)} fusion(bf16[2048,2048]{1,0:T(8,128)(2,1)S(1)} %bitcast.123, f32[2048]{0:T(1024)S(1)} %copy-done.24, f32[512,2048]{1,0:T(8,128)S(1)} %copy-done.18, f32[512]{0:T(512)S(1)} %add_sqrt_fusion), kind=kOutput, calls=%fused_computation.33 | convolution fusion | flops 4299161600 | bytes 14690304 | tf_op jit(solution)/shard_map/dot_general | solution.py:128
  355.0 11.0 %all-gather.16.cloned.1.call-done = f32[4,16,128,128]{3,2,1,0:T(8,128)} async-done(((f32[1,16,128,128]{3,2,1,0:T(8,128)}), f32[4,16,128,128]{3,2,1,0:T(8,128)}) %all-gather.16.cloned.1.call-update) | async-done | bytes 4194320 | tf_op jit(solution)/shard_map/all_gather | solution.py:24
  365.9 5.5 %fusion.29 = bf16[16,128,128]{2,1,0:T(8,128)(2,1)S(1)} fusion(f32[4,16,128,128]{3,2,1,0:T(8,128)} %all-gather.16.cloned.1.call-done, f32[16,128,128]{2,1,0:T(8,128)S(1)} %copy-done.19, f32[64,128,128]{2,1,0:T(8,128)} %all-gather.24.cloned.1.call-done, f32[32,128,128]{2,1,0:T(8,128)} %all-gather.20.cloned.1.call-done, pred[]{:T(512)S(6)} %lt.37, pred[]{:T(512)S(6)} %lt.38, ...), kind=kLoop, calls=%fused_computation.52 | loop fusion | flops 5767168 | bytes 12058634 | tf_op jit(solution)/shard_map/convert_element_type | solution.py:139
  371.5 3.3 convolution_add_fusion
  374.8 5.5 %copy.74 = f32[1,512,2048]{2,1,0:T(8,128)} copy(f32[1,512,2048]{1,2,0:T(8,128)} %bitcast.114) | data formatting | bytes 8388608 | tf_op jit(solution)/shard_map/reshape | solution.py:146
  380.4 7.3 %fusion.6 = (bf16[1,512,2048]{2,1,0:T(8,128)(2,1)}, bf16[1,512,2048]{2,1,0:T(8,128)(2,1)}) fusion(f32[1,512,2048]{2,1,0:T(8,128)} %copy.69, bf16[1,512,2048]{2,1,0:T(8,128)(2,1)} %param.6, f32[1,512,2048]{2,1,0:T(8,128)} %copy.74, bf16[1,512,2048]{2,1,0:T(8,128)(2,1)S(1)} %copy-done.21), kind=kLoop, calls=%fused_computation.15 | loop fusion | flops 20971520 | bytes 16777216 | tf_op jit(solution)/shard_map/convert_element_type | solution.py:143
  387.6 60.7 %reduce-scatter.7.cloned.1.call-done = bf16[1,64,2048]{2,1,0:T(8,128)(2,1)} async-done(((bf16[16,64,2048]{2,1,0:T(8,128)(2,1)}), bf16[1,64,2048]{2,1,0:T(8,128)(2,1)}) %reduce-scatter.7.cloned.1.call-update) | async-done | bytes 262160
  448.3 4.8 %all-to-all-start = ((bf16[4,16,2048]{2,1,0:T(8,128)(2,1)}), bf16[4,16,2048]{2,1,0:T(8,128)(2,1)S(1)}, u32[]{:S(2)}, u32[]{:S(2)}) async-start(bf16[4,16,2048]{2,1,0:T(8,128)(2,1)} %bitcast.120), calls=%async_computation.1 | async-start | bytes 524288 | tf_op jit(solution)/shard_map/all_to_all | solution.py:51
  453.1 5.1 %add_convert_fusion = bf16[16,128,512]{2,1,0:T(8,128)(2,1)} fusion(f32[16,128,512]{2,1,0:T(8,128)} %fusion.40, bf16[16,128,128]{2,1,0:T(8,128)(2,1)S(1)} %copy-done.23, bf16[512,16,128]{2,0,1:T(8,128)(2,1)} %copy-done.9), kind=kOutput, calls=%fused_computation.25 | convolution fusion | flops 270532608 | bytes 8912896 | tf_op jit(solution)/shard_map/while/body/eval_jaxpr/jhd,hde->jhe/dot_general | solution.py:72
  458.2 3.9 copy.78
  (77 shorter events, 6.1 us)
Async XLA Ops:
  7.2 201.5 %copy-start = (bf16[1,512,2048]{2,1,0:T(8,128)(2,1)S(1)}, bf16[1,512,2048]{2,1,0:T(8,128)(2,1)}, u32[]{:S(2)}) copy-start(bf16[1,512,2048]{2,1,0:T(8,128)(2,1)} %param.9) | copy-start | bytes 6291460
  7.2 25.2 %all-gather.18.cloned.1.call-start = ((), (), s32[]{:S(2)}) async-start(), calls=%async_computation.7 | async-start | bytes 3145728 | tf_op jit(solution)/shard_map/all_gather | solution.py:24
  7.2 2.4 copy-start.20
  9.6 3.1 copy-start.12
  12.7 1.3 copy-start.9
  16.5 68.4 %all-gather.22.cloned.1.call-start = ((), (), s32[]{:S(2)}) async-start(), calls=%async_computation.9 | async-start | bytes 5242880 | tf_op jit(solution)/shard_map/all_gather | solution.py:24
  35.0 101.9 %all-gather.12.cloned.1.call-start = ((), (), s32[]{:S(2)}) async-start(), calls=%async_computation.3 | async-start | bytes 5242880 | tf_op jit(solution)/shard_map/all_gather | solution.py:24
  88.3 120.4 %all-gather.14.cloned.1.call-start = ((), (), s32[]{:S(2)}) async-start(), calls=%async_computation.4 | async-start | bytes 8454144 | tf_op jit(solution)/shard_map/all_gather | solution.py:122
  88.9 151.4 %all-gather.20.cloned.1.call-start = ((), (), s32[]{:S(2)}) async-start(), calls=%async_computation.8 | async-start | bytes 3145728 | tf_op jit(solution)/shard_map/all_gather | solution.py:24
  92.5 3.1 copy-start.10
  94.2 1.3 copy-start.5
  95.5 5.9 %copy-start.13 = (bf16[64,8,16,128]{3,2,1,0:T(8,128)(2,1)S(1)}, bf16[64,8,16,128]{3,2,1,0:T(8,128)(2,1)}, u32[]{:S(2)}) copy-start(bf16[64,8,16,128]{3,2,1,0:T(8,128)(2,1)} %copy-done.12) | copy-start | bytes 6291460
  98.0 3.5 copy-start.4
  136.9 5.9 %copy-start.6 = (bf16[512,16,128]{2,0,1:T(8,128)(2,1)S(1)}, bf16[512,16,128]{2,0,1:T(8,128)(2,1)}, u32[]{:S(2)}) copy-start(bf16[512,16,128]{2,0,1:T(8,128)(2,1)} %copy-done.5) | copy-start | bytes 6291460
  136.9 6.2 %copy-start.16 = (f32[16,512,128]{1,2,0:T(8,128)S(1)}, f32[16,512,128]{1,2,0:T(8,128)}, u32[]{:S(2)}) copy-start(f32[16,512,128]{1,2,0:T(8,128)} %fusion.19) | copy-start | bytes 12582916
  145.8 62.8 %copy-start.24 = (f32[2048]{0:T(1024)S(1)}, f32[2048]{0:T(1024)}, u32[]{:S(2)}) copy-start(f32[2048]{0:T(1024)} %param.11) | copy-start | bytes 24580
  208.7 9.3 %copy-start.17 = (f32[512,2048]{1,0:T(8,128)S(1)}, f32[512,2048]{1,0:T(8,128)}, u32[]{:S(2)}) copy-start(f32[512,2048]{1,0:T(8,128)} %copy.64) | copy-start | bytes 12582916
  228.1 64.7 %all-gather.24.cloned.1.call-start = ((), (), s32[]{:S(2)}) async-start(), calls=%async_computation.10 | async-start | bytes 5242880 | tf_op jit(solution)/shard_map/all_gather | solution.py:24
  243.0 71.7 %reduce-scatter.5.cloned.1.call-start = ((), (), s32[]{:S(2)}) async-start(), calls=%async_computation.6 | async-start | bytes 12582912 | tf_op jit(solution)/shard_map/reduce_scatter | solution.py:45
  261.5 53.3 %copy-start.8 = (bf16[512,2048]{0,1:T(8,128)(2,1)S(1)}, bf16[512,2048]{0,1:T(8,128)(2,1)}, u32[]{:S(2)}) copy-start(bf16[512,2048]{0,1:T(8,128)(2,1)} %copy.85) | copy-start | bytes 6291460
  261.5 104.4 %all-gather.16.cloned.1.call-start = ((), (), s32[]{:S(2)}) async-start(), calls=%async_computation.5 | async-start | bytes 5242880 | tf_op jit(solution)/shard_map/all_gather | solution.py:24
  296.4 152.0 %reduce-scatter.7.cloned.1.call-start = ((), (), s32[]{:S(2)}) async-start(), calls=%async_computation.11 | async-start | bytes 4456448
  314.8 4.6 copy-start.11
  319.4 4.9 %copy-start.2 = (bf16[16,512,512]{2,1,0:T(8,128)(2,1)}, bf16[16,512,512]{2,1,0:T(8,128)(2,1)S(1)}, u32[]{:S(2)}) copy-start(bf16[16,512,512]{2,1,0:T(8,128)(2,1)S(1)} %select_convert_fusion) | copy-start | bytes 25165828
  335.0 7.7 %copy-start.3 = (bf16[16,512,512]{2,1,0:T(8,128)(2,1)S(1)}, bf16[16,512,512]{2,1,0:T(8,128)(2,1)}, u32[]{:S(2)}) copy-start(bf16[16,512,512]{2,1,0:T(8,128)(2,1)} %copy-done.2) | copy-start | bytes 25165828
  335.0 8.7 %copy-start.7 = (bf16[512,16,128]{2,0,1:T(8,128)(2,1)S(1)}, bf16[512,16,128]{2,0,1:T(8,128)(2,1)}, u32[]{:S(2)}) copy-start(bf16[512,16,128]{2,0,1:T(8,128)(2,1)} %copy-done.5) | copy-start | bytes 6291460
  335.0 12.3 %slice-start = ((s8[8388608]{0:T(1024)(128)(4,1)}), s8[4194304]{0:T(1024)(128)(4,1)S(1)}, s32[]{:S(2)}) async-start(s8[8388608]{0:T(1024)(128)(4,1)} %bitcast.122), calls=%async_computation.12 | async-start | bytes 8388608
  343.7 3.6 copy-start.18
  343.7 5.5 %slice-start.1 = ((s8[8388608]{0:T(1024)(128)(4,1)}), s8[4194304]{0:T(1024)(128)(4,1)S(1)}, s32[]{:S(2)}) async-start(s8[8388608]{0:T(1024)(128)(4,1)} %bitcast.122), calls=%async_computation.13 | async-start | bytes 8388608
  349.2 16.8 %copy-start.19 = (f32[16,128,128]{2,1,0:T(8,128)S(1)}, f32[16,128,128]{2,1,0:T(8,128)}, u32[]{:S(2)}) copy-start(f32[16,128,128]{2,1,0:T(8,128)} %fusion.39) | copy-start | bytes 3145732
  355.0 16.5 %copy-start.14 = (bf16[64,8,16,128]{3,2,1,0:T(8,128)(2,1)S(1)}, bf16[64,8,16,128]{3,2,1,0:T(8,128)(2,1)}, u32[]{:S(2)}) copy-start(bf16[64,8,16,128]{3,2,1,0:T(8,128)(2,1)} %copy-done.12) | copy-start | bytes 6291460
  365.9 5.5 %copy-start.15 = (f32[16,128,512]{2,1,0:T(8,128)S(1)}, f32[16,128,512]{2,1,0:T(8,128)}, u32[]{:S(2)}) copy-start(f32[16,128,512]{2,1,0:T(8,128)} %fusion.38) | copy-start | bytes 12582916
  371.5 3.3 copy-start.22
  374.8 5.5 %copy-start.21 = (bf16[1,512,2048]{2,1,0:T(8,128)(2,1)S(1)}, bf16[1,512,2048]{2,1,0:T(8,128)(2,1)}, u32[]{:S(2)}) copy-start(bf16[1,512,2048]{2,1,0:T(8,128)(2,1)} %param.7) | copy-start | bytes 6291460
  380.3 72.8 %copy-start.23 = (bf16[16,128,128]{2,1,0:T(8,128)(2,1)S(1)}, bf16[16,128,128]{2,1,0:T(8,128)(2,1)}, u32[]{:S(2)}) copy-start(bf16[16,128,128]{2,1,0:T(8,128)(2,1)} %copy-done.22) | copy-start | bytes 1572868
  448.3 13.8 %all-to-all-start = ((bf16[4,16,2048]{2,1,0:T(8,128)(2,1)}), bf16[4,16,2048]{2,1,0:T(8,128)(2,1)S(1)}, u32[]{:S(2)}, u32[]{:S(2)}) async-start(bf16[4,16,2048]{2,1,0:T(8,128)(2,1)} %bitcast.120), calls=%async_computation.1 | async-start | bytes 524288 | tf_op jit(solution)/shard_map/all_to_all | solution.py:51
  453.1 9.7 %copy-start.1 = (bf16[1,512,2048]{2,1,0:T(8,128)(2,1)S(1)}, bf16[1,512,2048]{2,1,0:T(8,128)(2,1)}, u32[]{:S(2)}) copy-start(bf16[1,512,2048]{2,1,0:T(8,128)(2,1)} %param.9) | copy-start | bytes 6291460
Sparse Core Ops, SparseCore 0:
  16.6 15.7 all-gather.17
  35.1 49.6 all-gather.21
  88.4 48.3 all-gather.11
  139.9 68.7 all-gather.13
  228.2 12.0 all-gather.19
  243.2 49.6 all-gather.23
  295.3 19.4 reduce-scatter.4
  316.4 49.4 all-gather.15
  369.3 78.9 reduce-scatter.6
where the time goes:
time: 475 us; the launch traced here: 470 us
  waiting for transfers between devices  287 us (60%)
  matrix products  72.4 us (15%)
  local copies, waits for them, and re-layouts  47.3 us (10%)
  other arithmetic  42.3 us (9%)
  between operations  14.4 us (3%)
  starting transfers between devices  5.63 us (1%)
    all_gather x6, waiting for transfers between devices, entering(): pieces = lax.all_gather(total, axis)  151 us
    unnamed x10, waiting for transfers between devices  61.4 us
    all_gather x1, waiting for transfers between devices, shards(): full_weight = lax.all_gather(out_weight, SEQ_DP, axis=0, tiled=True)  57.2 us
    dot_general x10, matrix products, product(): return jnp.einsum(form, left, right, preferred_element_type=jnp.float32)  43.4 us
    reduce_scatter x1, waiting for transfers between devices, scatter_pairs(): blocks = lax.psum_scatter(blocks, core, scatter_dimension=0, tiled=True)  18.4 us
    unnamed x58, local copies, waits for them, and re-layouts  17.6 us
    add x4, other arithmetic, add_states(): return earlier + following  12.2 us
  transfers between devices with their start and end apart: 10, of which 9 were waited for; matrix products, arithmetic and copies ran while one was open for 25% of the time, Pallas kernels for 0%

commit v1 on v0

--- a/solution.py
+++ b/solution.py
@@ -119,7 +119,10 @@
     local_incl = jnp.cumsum(block_kv, axis=0)
     incoming = entering(local_incl[-1], SEQ, add_states, zero_state, False)
     prefix = (incoming[None] + (local_incl - block_kv)).astype(jnp.bfloat16)
-    full_weight = lax.all_gather(out_weight, SEQ_DP, axis=0, tiled=True)
+    peers_2 = lax.axis_size(SEQ_DP)
+    parts = jnp.stack([out_weight for _ in range(peers_2)])
+    parts = lax.all_to_all(parts, SEQ_DP, split_axis=0, concat_axis=0)
+    full_weight = jnp.concatenate(parts, axis=0)
     attention = lax.map(forward_only, (feat_query, feat_key, value_blocks, prefix))
     attention = attention.reshape(tokens, feature_count)
     radius = jnp.sqrt(jnp.mean(attention * attention, axis=-1, keepdims=True) + epsilon)

time: 475 us -> 512 us (1.078)
  waiting for transfers between devices: 287 us -> 308 us
  starting transfers between devices: 5.63 us -> 15.5 us
    all_gather x6, waiting for transfers between devices: 151 us -> 229 us  [entering(): pieces = lax.all_gather(total, axis)]
    all_gather x1 -> x0, waiting for transfers between devices: 57.2 us -> none  [shards(): full_weight = lax.all_gather(out_weight, SEQ_DP, axis=0, tiled=True)]
    all_to_all x0 -> x1, starting transfers between devices: none -> 9.89 us  [shards(): parts = lax.all_to_all(parts, SEQ_DP, split_axis=0, concat_axis=0)]
    unnamed x10 -> x9, waiting for transfers between devices: 61.4 us -> 60.8 us
  transfers between devices with their start and end apart: 10 -> 10, of which waited for: 9 -> 8; matrix products, arithmetic and copies ran while one was open for 25% -> 25% of each run, Pallas kernels for 0% -> 0%
where the time goes in v1:
time: 512 us; the launch traced here: 506 us
  waiting for transfers between devices  308 us (60%)
  matrix products  75.8 us (15%)
  local copies, waits for them, and re-layouts  50 us (10%)
  other arithmetic  42.3 us (8%)
  starting transfers between devices  15.5 us (3%)
  between operations  14.7 us (3%)
    all_gather x6, waiting for transfers between devices, entering(): pieces = lax.all_gather(total, axis)  229 us
    unnamed x9, waiting for transfers between devices  60.8 us
    dot_general x10, matrix products, product(): return jnp.einsum(form, left, right, preferred_element_type=jnp.float32)  43.5 us
    reduce_scatter x1, waiting for transfers between devices, scatter_pairs(): blocks = lax.psum_scatter(blocks, core, scatter_dimension=0, tiled=True)  18.2 us
    unnamed x58, local copies, waits for them, and re-layouts  15.8 us
    add x4, other arithmetic, add_states(): return earlier + following  12.2 us
  transfers between devices with their start and end apart: 10, of which 8 were waited for; matrix products, arithmetic and copies ran while one was open for 25% of the time, Pallas kernels for 0%

profile of v1, /device:TPU:2, one launch (start us, length us, event | category | flops | bytes accessed | tf_op | source)
XLA Modules:
  0.0 506.0 jit_solution(9683974608476083310)
XLA Ops:
  7.2 2.3 copy.88
  11.1 1.6 multiply_convert_fusion.1
  12.7 1.3 copy-done.9
  14.1 2.4 fusion.22
  16.6 15.8 %all-gather.15.cloned.1.call-done = f32[32,128,128]{2,1,0:T(8,128)} async-done(((f32[16,128,128]{2,1,0:T(8,128)}), f32[32,128,128]{2,1,0:T(8,128)}) %all-gather.15.cloned.1.call-update) | async-done | bytes 2097168 | tf_op jit(solution)/shard_map/all_gather | solution.py:24
  32.4 2.6 slice_add_fusion.13
  35.1 4.3 stack.2
  39.4 9.9 %all-to-all-start = ((bf16[128,16,2048]{2,1,0:T(8,128)(2,1)}), bf16[128,16,2048]{2,1,0:T(8,128)(2,1)}, u32[]{:S(2)}, u32[]{:S(2)}) async-start(bf16[128,16,2048]{2,1,0:T(8,128)(2,1)} %stack.2), calls=%async_computation | async-start | bytes 16777216 | tf_op jit(solution)/shard_map/all_to_all | solution.py:124
  49.4 126.8 %all-gather.19.cloned.1.call-done = f32[64,128,128]{2,1,0:T(8,128)} async-done(((f32[16,128,128]{2,1,0:T(8,128)}), f32[64,128,128]{2,1,0:T(8,128)}) %all-gather.19.cloned.1.call-update) | async-done | bytes 4194320 | tf_op jit(solution)/shard_map/all_gather | solution.py:24
  176.2 3.4 fusion.35
  180.2 2.1 convert_bitcast_fusion.1
  183.4 1.6 multiply_convert_fusion.2
  185.0 1.3 copy-done.5
  186.3 2.5 select_convert_fusion.1
  188.8 3.6 copy-done.4
  192.4 5.0 fusion.18
  197.3 31.4 %all-gather.11.cloned.1.call-done = f32[4,16,128,128]{3,2,1,0:T(8,128)} async-done(((f32[1,16,128,128]{3,2,1,0:T(8,128)}), f32[4,16,128,128]{3,2,1,0:T(8,128)}) %all-gather.11.cloned.1.call-update) | async-done | bytes 4194320 | tf_op jit(solution)/shard_map/all_gather | solution.py:24
  228.7 5.8 %fusion.34 = bf16[16,128,128]{2,1,0:T(8,128)(2,1)S(1)} fusion(f32[4,16,128,128]{3,2,1,0:T(8,128)} %all-gather.11.cloned.1.call-done, f32[16,128,128]{2,1,0:T(8,128)} %fusion.22, f32[64,128,128]{2,1,0:T(8,128)} %all-gather.19.cloned.1.call-done, f32[32,128,128]{2,1,0:T(8,128)} %all-gather.15.cloned.1.call-done, pred[]{:T(512)S(6)} %gt.35, pred[]{:T(512)S(6)} %gt.36, ...), kind=kLoop, calls=%fused_computation.63 | loop fusion | flops 5767168 | bytes 12058634 | tf_op jit(solution)/shard_map/convert_element_type | solution.py:121
  234.9 2.8 multiply_reduce_fusion.1
  237.7 5.5 %copy.64 = f32[512,2048]{1,0:T(8,128)} copy(f32[512,2048]{0,1:T(8,128)} %bitcast.108) | data formatting | bytes 8388608 | tf_op jit(solution)/shard_map/reshape | solution.py:127
  243.3 9.3 %multiply_reduce_fusion = (f32[512]{0:T(512)S(1)}, f32[512,2048]{1,0:T(8,128)S(1)}) fusion(f32[2048]{0:T(1024)S(1)} %copy-done.26, f32[512,2048]{1,0:T(8,128)} %copy.64, f32[512]{0:T(512)S(1)} %add_sqrt_fusion, bf16[2048,2048]{1,0:T(8,128)(2,1)} %bitcast.8, bf16[1,512,2048]{2,1,0:T(8,128)(2,1)S(1)} %copy-done), kind=kOutput, calls=%fused_computation.26 | convolution fusion | flops 4299161088 | bytes 18886656 | tf_op jit(solution)/shard_map/dot_general | solution.py:133
  252.6 2.2 divide_convert_fusion
  254.9 3.9 copy.85
  258.8 4.0 fusion.38
  262.8 13.8 %all-gather.17.cloned.1.call-done = f32[32,128,128]{2,1,0:T(8,128)} async-done(((f32[16,128,128]{2,1,0:T(8,128)}), f32[32,128,128]{2,1,0:T(8,128)}) %all-gather.17.cloned.1.call-update) | async-done | bytes 2097168 | tf_op jit(solution)/shard_map/all_gather | solution.py:24
  276.6 2.7 slice_add_fusion.6
  279.3 2.6 multiply_convert_fusion
  282.0 6.8 %convolution_convert_fusion = bf16[2048,2048]{1,0:T(8,128)(2,1)} fusion(bf16[512,2048]{0,1:T(8,128)(2,1)S(1)} %bitcast.120, bf16[1,512,2048]{2,1,0:T(8,128)(2,1)S(1)} %copy-done), kind=kOutput, calls=%fused_computation.2 | convolution fusion | flops 4299161600 | bytes 12582912 | tf_op jit(solution)/shard_map/dot_general | solution.py:152
  288.7 9.0 %copy.77 = bf16[16,2,64,2048]{3,2,0,1:T(8,128)(2,1)} copy(bf16[16,2,64,2048]{3,2,1,0:T(8,128)(2,1)} %bitcast.119) | data formatting | bytes 16777216 | tf_op jit(solution)/shard_map/reshape;reshape | solution.py:44
  297.8 31.3 %all-gather.21.cloned.1.call-done = f32[64,128,128]{2,1,0:T(8,128)} async-done(((f32[16,128,128]{2,1,0:T(8,128)}), f32[64,128,128]{2,1,0:T(8,128)}) %all-gather.21.cloned.1.call-update) | async-done | bytes 4194320 | tf_op jit(solution)/shard_map/all_gather | solution.py:24
  329.1 3.4 fusion.29
  332.7 18.2 %reduce-scatter.5.cloned.1.call-done = bf16[16,64,2048]{2,1,0:T(8,128)(2,1)} async-done(((bf16[32,64,2048]{2,1,0:T(8,128)(2,1)}), bf16[16,64,2048]{2,1,0:T(8,128)(2,1)}) %reduce-scatter.5.cloned.1.call-update) | async-done | bytes 4194320 | tf_op jit(solution)/shard_map/reduce_scatter | solution.py:45
  350.9 4.6 select_convert_fusion
  355.6 4.9 fusion.36
  360.4 4.9 convolution_add_fusion.1
  365.4 5.8 %copy.69 = f32[1,512,2048]{2,1,0:T(8,128)} copy(f32[1,512,2048]{1,2,0:T(8,128)} %bitcast.115) | data formatting | bytes 8388608 | tf_op jit(solution)/shard_map/reshape | solution.py:146
  371.1 7.7 %fusion.39 = f32[16,128,512]{2,1,0:T(8,128)} fusion(bf16[512,16,128]{0,2,1:T(8,128)(2,1)} %bitcast.105, bf16[16,512,512]{2,1,0:T(8,128)(2,1)} %copy-done.4), kind=kOutput, calls=%fused_computation.82 | convolution fusion | flops 1073741824 | bytes 14680064 | tf_op jit(solution)/shard_map/while/body/eval_jaxpr/hij,ihe->jhe/dot_general | solution.py:72
  379.8 3.4 fusion.37
  383.3 9.3 %fusion.14 = bf16[1,512,2048]{2,1,0:T(8,128)(2,1)} fusion(bf16[512,2048]{0,1:T(8,128)(2,1)S(1)} %bitcast.121, bf16[2048,2048]{1,0:T(8,128)(2,1)} %bitcast.8), kind=kOutput, calls=%fused_computation.32 | convolution fusion | flops 4296015872 | bytes 12582912 | tf_op jit(solution)/shard_map/dot_general | solution.py:131
  392.5 9.5 %all-gather.13.cloned.1.call-done = f32[4,16,128,128]{3,2,1,0:T(8,128)} async-done(((f32[1,16,128,128]{3,2,1,0:T(8,128)}), f32[4,16,128,128]{3,2,1,0:T(8,128)}) %all-gather.13.cloned.1.call-update) | async-done | bytes 4194320 | tf_op jit(solution)/shard_map/all_gather | solution.py:24
  402.1 5.5 %fusion.28 = bf16[16,128,128]{2,1,0:T(8,128)(2,1)S(1)} fusion(f32[4,16,128,128]{3,2,1,0:T(8,128)} %all-gather.13.cloned.1.call-done, f32[16,128,128]{2,1,0:T(8,128)S(1)} %copy-done.18, f32[64,128,128]{2,1,0:T(8,128)} %all-gather.21.cloned.1.call-done, f32[32,128,128]{2,1,0:T(8,128)} %all-gather.17.cloned.1.call-done, pred[]{:T(512)S(6)} %lt.37, pred[]{:T(512)S(6)} %lt.38, ...), kind=kLoop, calls=%fused_computation.50 | loop fusion | flops 5767168 | bytes 12058634 | tf_op jit(solution)/shard_map/convert_element_type | solution.py:142
  407.6 3.3 convolution_add_fusion
  411.0 5.6 %copy.74 = f32[1,512,2048]{2,1,0:T(8,128)} copy(f32[1,512,2048]{1,2,0:T(8,128)} %bitcast.116) | data formatting | bytes 8388608 | tf_op jit(solution)/shard_map/reshape | solution.py:149
  416.5 7.3 %fusion.6 = (bf16[1,512,2048]{2,1,0:T(8,128)(2,1)}, bf16[1,512,2048]{2,1,0:T(8,128)(2,1)}) fusion(f32[1,512,2048]{2,1,0:T(8,128)} %copy.69, bf16[1,512,2048]{2,1,0:T(8,128)(2,1)} %param.6, f32[1,512,2048]{2,1,0:T(8,128)} %copy.74, bf16[1,512,2048]{2,1,0:T(8,128)(2,1)S(1)} %copy-done.20), kind=kLoop, calls=%fused_computation.15 | loop fusion | flops 20971520 | bytes 16777216 | tf_op jit(solution)/shard_map/convert_element_type | solution.py:146
  423.8 60.6 %reduce-scatter.7.cloned.1.call-done = bf16[1,64,2048]{2,1,0:T(8,128)(2,1)} async-done(((bf16[16,64,2048]{2,1,0:T(8,128)(2,1)}), bf16[1,64,2048]{2,1,0:T(8,128)(2,1)}) %reduce-scatter.7.cloned.1.call-update) | async-done | bytes 262160
  484.4 4.8 all-to-all-start.1
  489.2 5.1 %add_convert_fusion = bf16[16,128,512]{2,1,0:T(8,128)(2,1)} fusion(f32[16,128,512]{2,1,0:T(8,128)} %fusion.39, bf16[16,128,128]{2,1,0:T(8,128)(2,1)S(1)} %copy-done.22, bf16[512,16,128]{2,0,1:T(8,128)(2,1)} %copy-done.9), kind=kOutput, calls=%fused_computation.24 | convolution fusion | flops 270532608 | bytes 8912896 | tf_op jit(solution)/shard_map/while/body/eval_jaxpr/jhd,hde->jhe/dot_general | solution.py:72
  494.3 3.9 copy.78
  (76 shorter events, 5.6 us)
Async XLA Ops:
  7.2 236.1 %copy-start = (bf16[1,512,2048]{2,1,0:T(8,128)(2,1)S(1)}, bf16[1,512,2048]{2,1,0:T(8,128)(2,1)}, u32[]{:S(2)}) copy-start(bf16[1,512,2048]{2,1,0:T(8,128)(2,1)} %param.9) | copy-start | bytes 6291460
  7.2 25.2 %all-gather.15.cloned.1.call-start = ((), (), s32[]{:S(2)}) async-start(), calls=%async_computation.7 | async-start | bytes 3145728 | tf_op jit(solution)/shard_map/all_gather | solution.py:24
  7.2 2.4 copy-start.19
  9.6 3.1 copy-start.12
  12.7 1.4 copy-start.9
  14.1 21.0 %copy-start.25 = (bf16[16,2048]{1,0:T(8,128)(2,1)S(1)}, bf16[16,2048]{1,0:T(8,128)(2,1)}, u32[]{:S(2)}) copy-start(bf16[16,2048]{1,0:T(8,128)(2,1)} %param.10) | copy-start | bytes 196612
  16.5 159.7 %all-gather.19.cloned.1.call-start = ((), (), s32[]{:S(2)}) async-start(), calls=%async_computation.9 | async-start | bytes 5242880 | tf_op jit(solution)/shard_map/all_gather | solution.py:24
  39.4 203.9 %all-to-all-start = ((bf16[128,16,2048]{2,1,0:T(8,128)(2,1)}), bf16[128,16,2048]{2,1,0:T(8,128)(2,1)}, u32[]{:S(2)}, u32[]{:S(2)}) async-start(bf16[128,16,2048]{2,1,0:T(8,128)(2,1)} %stack.2), calls=%async_computation | async-start | bytes 16777216 | tf_op jit(solution)/shard_map/all_to_all | solution.py:124
  49.3 179.4 %all-gather.11.cloned.1.call-start = ((), (), s32[]{:S(2)}) async-start(), calls=%async_computation.4 | async-start | bytes 5242880 | tf_op jit(solution)/shard_map/all_gather | solution.py:24
  179.7 96.9 %all-gather.17.cloned.1.call-start = ((), (), s32[]{:S(2)}) async-start(), calls=%async_computation.8 | async-start | bytes 3145728 | tf_op jit(solution)/shard_map/all_gather | solution.py:24
  183.3 3.1 copy-start.10
  185.0 1.3 copy-start.5
  186.3 6.0 %copy-start.13 = (bf16[64,8,16,128]{3,2,1,0:T(8,128)(2,1)S(1)}, bf16[64,8,16,128]{3,2,1,0:T(8,128)(2,1)}, u32[]{:S(2)}) copy-start(bf16[64,8,16,128]{3,2,1,0:T(8,128)(2,1)} %copy-done.12) | copy-start | bytes 6291460
  188.8 3.6 copy-start.4
  228.7 5.9 %copy-start.6 = (bf16[512,16,128]{2,0,1:T(8,128)(2,1)S(1)}, bf16[512,16,128]{2,0,1:T(8,128)(2,1)}, u32[]{:S(2)}) copy-start(bf16[512,16,128]{2,0,1:T(8,128)(2,1)} %copy-done.5) | copy-start | bytes 6291460
  228.7 6.2 %copy-start.16 = (f32[16,512,128]{1,2,0:T(8,128)S(1)}, f32[16,512,128]{1,2,0:T(8,128)}, u32[]{:S(2)}) copy-start(f32[16,512,128]{1,2,0:T(8,128)} %fusion.18) | copy-start | bytes 12582916
  237.7 5.6 %copy-start.26 = (f32[2048]{0:T(1024)S(1)}, f32[2048]{0:T(1024)}, u32[]{:S(2)}) copy-start(f32[2048]{0:T(1024)} %param.11) | copy-start | bytes 24580
  243.3 9.3 %copy-start.17 = (f32[512,2048]{1,0:T(8,128)S(1)}, f32[512,2048]{1,0:T(8,128)}, u32[]{:S(2)}) copy-start(f32[512,2048]{1,0:T(8,128)} %copy.64) | copy-start | bytes 12582916
  262.8 66.4 %all-gather.21.cloned.1.call-start = ((), (), s32[]{:S(2)}) async-start(), calls=%async_computation.10 | async-start | bytes 5242880 | tf_op jit(solution)/shard_map/all_gather | solution.py:24
  279.3 71.6 %reduce-scatter.5.cloned.1.call-start = ((), (), s32[]{:S(2)}) async-start(), calls=%async_computation.6 | async-start | bytes 12582912 | tf_op jit(solution)/shard_map/reduce_scatter | solution.py:45
  282.0 6.8 %copy-start.23 = (bf16[512,16,128]{0,2,1:T(8,128)(2,1)}, bf16[512,16,128]{0,2,1:T(8,128)(2,1)S(1)}, u32[]{:S(2)}) copy-start(bf16[512,16,128]{0,2,1:T(8,128)(2,1)S(1)} %multiply_convert_fusion) | copy-start | bytes 6291460
  297.8 53.2 %copy-start.8 = (bf16[512,2048]{0,1:T(8,128)(2,1)S(1)}, bf16[512,2048]{0,1:T(8,128)(2,1)}, u32[]{:S(2)}) copy-start(bf16[512,2048]{0,1:T(8,128)(2,1)} %copy.85) | copy-start | bytes 6291460
  297.8 104.3 %all-gather.13.cloned.1.call-start = ((), (), s32[]{:S(2)}) async-start(), calls=%async_computation.5 | async-start | bytes 5242880 | tf_op jit(solution)/shard_map/all_gather | solution.py:24
  332.6 151.8 %reduce-scatter.7.cloned.1.call-start = ((), (), s32[]{:S(2)}) async-start(), calls=%async_computation.11 | async-start | bytes 4456448
  350.9 4.6 copy-start.11
  355.6 4.9 copy-start.2
  371.1 7.7 %copy-start.3 = (bf16[16,512,512]{2,1,0:T(8,128)(2,1)S(1)}, bf16[16,512,512]{2,1,0:T(8,128)(2,1)}, u32[]{:S(2)}) copy-start(bf16[16,512,512]{2,1,0:T(8,128)(2,1)} %copy-done.2) | copy-start | bytes 25165828
  371.1 8.7 %copy-start.7 = (bf16[512,16,128]{2,0,1:T(8,128)(2,1)S(1)}, bf16[512,16,128]{2,0,1:T(8,128)(2,1)}, u32[]{:S(2)}) copy-start(bf16[512,16,128]{2,0,1:T(8,128)(2,1)} %copy-done.5) | copy-start | bytes 6291460
  379.8 3.4 copy-start.24
  383.3 18.8 %copy-start.18 = (f32[16,128,128]{2,1,0:T(8,128)S(1)}, f32[16,128,128]{2,1,0:T(8,128)}, u32[]{:S(2)}) copy-start(f32[16,128,128]{2,1,0:T(8,128)} %fusion.38) | copy-start | bytes 3145732
  392.5 15.1 %copy-start.14 = (bf16[64,8,16,128]{3,2,1,0:T(8,128)(2,1)S(1)}, bf16[64,8,16,128]{3,2,1,0:T(8,128)(2,1)}, u32[]{:S(2)}) copy-start(bf16[64,8,16,128]{3,2,1,0:T(8,128)(2,1)} %copy-done.12) | copy-start | bytes 6291460
  402.1 5.5 %copy-start.15 = (f32[16,128,512]{2,1,0:T(8,128)S(1)}, f32[16,128,512]{2,1,0:T(8,128)}, u32[]{:S(2)}) copy-start(f32[16,128,512]{2,1,0:T(8,128)} %fusion.37) | copy-start | bytes 12582916
  407.6 3.3 copy-start.21
  411.0 5.6 %copy-start.20 = (bf16[1,512,2048]{2,1,0:T(8,128)(2,1)S(1)}, bf16[1,512,2048]{2,1,0:T(8,128)(2,1)}, u32[]{:S(2)}) copy-start(bf16[1,512,2048]{2,1,0:T(8,128)(2,1)} %param.7) | copy-start | bytes 6291460
  416.5 72.7 %copy-start.22 = (bf16[16,128,128]{2,1,0:T(8,128)(2,1)S(1)}, bf16[16,128,128]{2,1,0:T(8,128)(2,1)}, u32[]{:S(2)}) copy-start(bf16[16,128,128]{2,1,0:T(8,128)(2,1)} %copy-done.21) | copy-start | bytes 1572868
  484.4 13.8 %all-to-all-start.1 = ((bf16[4,16,2048]{2,1,0:T(8,128)(2,1)}), bf16[4,16,2048]{2,1,0:T(8,128)(2,1)S(1)}, u32[]{:S(2)}, u32[]{:S(2)}) async-start(bf16[4,16,2048]{2,1,0:T(8,128)(2,1)} %bitcast.123), calls=%async_computation.2 | async-start | bytes 524288 | tf_op jit(solution)/shard_map/all_to_all | solution.py:51
  489.2 9.7 %copy-start.1 = (bf16[1,512,2048]{2,1,0:T(8,128)(2,1)S(1)}, bf16[1,512,2048]{2,1,0:T(8,128)(2,1)}, u32[]{:S(2)}) copy-start(bf16[1,512,2048]{2,1,0:T(8,128)(2,1)} %param.9) | copy-start | bytes 6291460
Sparse Core Ops, SparseCore 0:
  16.6 15.6 all-gather.14
  35.2 140.9 all-gather.18
  179.8 48.8 all-gather.10
  262.9 13.6 all-gather.16
  279.4 49.6 all-gather.20
  331.4 19.4 reduce-scatter.4
  352.5 49.4 all-gather.12
  405.4 78.9 reduce-scatter.6
